TPU v7x, 32 devices: a whole 2x2x4 slice. The times are simulated.
32 devices in a mesh: data: 32 (over z, y, x, core).
Axes of the slice: x: 2, y: 2, z: 4, core: 2. Of those that a mesh axis runs over, the one named last changes fastest.
Arguments:
- h_a: bfloat16 [16384, 2048], P('data')
- h_b: bfloat16 [16384, 2048], P('data')
- w_one: bfloat16 [2048, 2048], replicated
- w_two: bfloat16 [2048, 2048], replicated
- w_three: bfloat16 [2048, 2048], replicated
- gain_one: float32 [2048], replicated
- shift_one: float32 [2048], replicated
- gain_two: float32 [2048], replicated
- shift_two: float32 [2048], replicated
- lam_off: float32 [], replicated
Outputs:
- output 1: float32 [], replicated
- output 2: float32 [2048, 2048], P('data')
- output 3: float32 [2048, 2048], P('data')
- output 4: float32 [2048, 2048], P('data')
- output 5: float32 [2048], replicated
- output 6: float32 [2048], replicated
- output 7: float32 [2048], replicated
- output 8: float32 [2048], replicated
All inputs are finite; a program needn't handle non-finite values.
Results may differ from a plain program's by a relative error of at most 0.00508914.
Values are sent between devices in bfloat16 or wider.
A program may use at most 1 GiB of HBM per device.

v0:
```python
import functools

import jax
import jax.numpy as jnp
from jax import lax
from jax.experimental import pallas as pl
from jax.experimental.pallas import tpu as pltpu
from jax.sharding import PartitionSpec as P

NORM_EPS = 1e-5
MESH = pl.DeviceIdType.MESH
F32 = jnp.float32
BF16 = jnp.bfloat16


ALL = slice(None)
FIRST, SECOND, THIRD, FOURTH = [slice(k, k + 1) for k in range(4)]
PAIR = range(2)
OTHERS = range(3)
LINE = 4
CUBE = 8
DEPTH_DIMS = (((0,), (0,)), ((), ()))
LANE_DIMS = (((1,), (1,)), ((), ()))
DMA_SEM = pltpu.SemaphoreType.DMA


def loop(count):
    return pl.loop(0, count)


def col_sum(values):
    return jnp.sum(values, axis=0, keepdims=True)


class Place:
    def __init__(self):
        me = lax.axis_index("data")
        self.core = lax.rem(me, 2)
        self.x = lax.rem(lax.div(me, 2), 2)
        self.y = lax.rem(lax.div(me, 4), 2)
        self.z = lax.div(me, 8)
        self.plane = lax.rem(lax.div(me, 2), 4)
        self.partner = me + 1 - 2 * self.core
        self.x_peer = me + 2 - 4 * self.x
        self.y_peer = me + 4 - 8 * self.y
        self.low = lax.rem(me, CUBE)
        self.others = [lax.rem(self.z + d + 1, LINE) for d in OTHERS]
        self.z_peers = [z * CUBE + self.low for z in self.others]
        self.plane_peers = [self.z * CUBE + lax.rem(self.plane + d + 1, LINE) * 2 + self.core for d in OTHERS]
        self.cube_peers = [self.z * CUBE + lax.rem(self.low + d + 1, CUBE) for d in range(CUBE - 1)]
        self.near = [self.partner] + self.plane_peers + self.z_peers


def enter(peers):
    barrier = pltpu.get_barrier_semaphore()
    for peer in peers:
        pl.semaphore_signal(barrier, inc=1, device_id=(peer,), device_id_type=MESH)
    pl.semaphore_wait(barrier, len(peers))


def remote(src, dst, send_sem, recv_sem, peer):
    return pltpu.make_async_remote_copy(
        src_ref=src, dst_ref=dst, send_sem=send_sem, recv_sem=recv_sem,
        device_id=(peer,), device_id_type=MESH)


class Sums:
    def __init__(self, at, local, total, recv0, slots1, slots2, send_sem, recv_sem):
        self.at, self.refs = at, (local, total)
        self.recv0, self.slots1, self.slots2 = recv0, slots1, slots2
        self.send_sem, self.recv_sem = send_sem, recv_sem
        self.half = recv0.shape[-1]
        self.mine = pl.multiple_of(at.core * self.half, 128)
        self.theirs = pl.multiple_of((1 - at.core) * self.half, 128)

    def pick(self, k, first):
        ref, index = self.refs[k]
        return ref.at[(*index, ALL, pl.ds(first, self.half))]

    def copies(self, stage):
        at = self.at
        if stage == 0:
            pairs = [(0, self.pick(0, self.theirs), self.recv0, at.partner)]
        elif stage == 1:
            here = self.slots1.at[at.plane]
            pairs = [(1 + d, here, here, at.plane_peers[d]) for d in OTHERS]
        elif stage == 2:
            here = self.slots2.at[at.z]
            pairs = [(4 + d, here, here, at.z_peers[d]) for d in OTHERS]
        else:
            here = self.pick(1, self.mine)
            pairs = [(7, here, here, at.partner)]
        return [remote(src, dst, self.send_sem.at[k], self.recv_sem.at[k], peer) for k, src, dst, peer in pairs]

    def send(self, stage):
        for copy in self.copies(stage):
            copy.start()

    def arrive(self, stage=3):
        for copy in self.copies(stage):
            copy.wait()

    def begin(self):
        self.send(0)

    def over_plane(self):
        self.arrive(0)
        self.slots1[self.at.plane] = self.pick(0, self.mine)[...] + self.recv0[...]
        self.send(1)

    def over_line(self):
        self.arrive(1)
        self.slots2[self.at.z] = jnp.sum(self.slots1[...], axis=0)
        self.send(2)

    def over_pair(self):
        self.arrive(2)
        self.pick(1, self.mine)[...] = jnp.sum(self.slots2[...], axis=0)
        self.send(3)


class QuickSums:
    def __init__(self, at, local, total, slots1, slots2, send_sem, recv_sem):
        self.at, self.local, self.total = at, local, total
        self.slots1, self.slots2 = slots1, slots2
        self.send_sem, self.recv_sem = send_sem, recv_sem

    def copies(self, across):
        at = self.at
        if across:
            here, peers, first = self.slots2.at[at.low], at.cube_peers, len(at.z_peers)
        else:
            here, peers, first = self.slots1.at[at.z], at.z_peers, 0
        return [remote(here, here, self.send_sem.at[first + d], self.recv_sem.at[first + d], peer)
                for d, peer in enumerate(peers)]

    def begin(self):
        ref, index = self.local
        self.slots1[self.at.z] = ref[index]
        for copy in self.copies(False):
            copy.start()

    def over_plane(self):
        for copy in self.copies(False):
            copy.wait()
        self.slots2[self.at.low] = jnp.sum(self.slots1[...], axis=0)
        for copy in self.copies(True):
            copy.start()

    def arrive(self):
        for copy in self.copies(True):
            copy.wait()
        ref, index = self.total
        ref[index] = jnp.sum(self.slots2[...], axis=0)


def quick_scratch(rows, cols):
    return [
        pltpu.VMEM((LINE, rows, cols), F32),
        pltpu.VMEM((CUBE, rows, cols), F32),
        DMA_SEM((LINE + CUBE,)),
        DMA_SEM((LINE + CUBE,)),
    ]


def sums_scratch(rows, cols):
    return [
        pltpu.VMEM((rows, cols // 2), F32),
        pltpu.VMEM((4, rows, cols // 2), F32),
        pltpu.VMEM((4, rows, cols // 2), F32),
        DMA_SEM((8,)),
        DMA_SEM((8,)),
    ]


class Ring:
    def __init__(self, at, total, spread, part, recv0, kept, snd1, recv1, snd2, recv2, snd3, recv3, send_sem, recv_sem, credit):
        self.at, self.total, self.slots, self.spread = at, total, kept.shape[0], spread
        self.part, self.recv0, self.kept = part, recv0, kept
        self.snd1, self.recv1, self.snd2, self.recv2, self.snd3, self.recv3 = snd1, recv1, snd2, recv2, snd3, recv3
        self.send_sem, self.recv_sem, self.credit = send_sem, recv_sem, credit
        self.half = snd1.shape[-1]
        self.peers = [at.partner, at.x_peer, at.y_peer, at.y_peer, at.x_peer] + at.z_peers
        self.givers = self.peers[:5] + at.z_peers[::-1]
        self.own = [at.y, at.x]

    def cols(self, half):
        return pl.ds(half * self.half, self.half)

    def copy(self, q, stage):
        j, s = lax.rem(q, self.slots), lax.rem(q, 2)
        if stage > 7:
            src, dst, peer = self.spread(q, stage)
        else:
            peer = self.peers[stage]
            if stage > 4:
                src, dst = self.snd3.at[j, stage - 5], self.recv3.at[j, stage - 5]
            elif stage > 2:
                src, dst = self.snd2.at[j, stage - 3], self.recv2.at[j, stage - 3]
            elif stage:
                src, dst = self.snd1.at[j, stage - 1], self.recv1.at[j, stage - 1]
            else:
                src, dst = self.part.at[s, :, :, :, 1 - self.at.core], self.recv0.at[s]
        return remote(src, dst, self.send_sem.at[j, stage], self.recv_sem.at[j, stage], peer)

    def start(self, q, *stages):
        for stage in stages:
            self.copy(q, stage).start()

    def wait(self, q, *stages):
        for stage in stages:
            self.copy(q, stage).wait()

    def depth(self, stage):
        return self.slots if stage else self.part.shape[0]

    def send(self, q, *stages):
        for stage in stages:
            depth = self.depth(stage)
            pl.when(q >= depth)(lambda: pl.semaphore_wait(self.credit.at[lax.rem(q, depth), stage], 1))
            self.start(q, stage)

    def give(self, q, *stages):
        for stage in stages:
            depth = self.depth(stage)
            pl.when(q + depth < self.total)(lambda: pl.semaphore_signal(
                self.credit.at[lax.rem(q, depth), stage], inc=1, device_id=(self.givers[stage],), device_id_type=MESH))

    def pair(self, q):
        self.send(q, 0)

    def first(self, q):
        at, s, j = self.at, lax.rem(q, 2), lax.rem(q, self.slots)
        self.wait(q, 0)

        @loop(LINE)
        def _(z):
            for half in PAIR:
                cols = self.cols(half)
                for k in PAIR:
                    (y, x), (oy, ox) = ((at.y, k), (1 - at.y, k)) if half else ((k, at.x), (k, 1 - at.x))
                    self.snd1[j, half, z, k] = (
                        self.part[s, z, oy, ox, at.core, :, cols] + self.recv0[s, z, oy, ox, :, cols]).astype(BF16)
                    self.kept[j, half, z, k] = self.part[s, z, y, x, at.core, :, cols] + self.recv0[s, z, y, x, :, cols]

        self.give(q, 0)
        self.send(q, 1, 2)

    def second(self, q):
        j = lax.rem(q, self.slots)
        for half in PAIR:
            own = self.own[half]
            self.wait(q, 1 + half)

            @loop(LINE)
            def _(z):
                self.snd2[j, half, z] = (
                    self.kept[j, half, z, 1 - own] + self.recv1[j, half, z, 1 - own].astype(F32)).astype(BF16)
                self.kept[j, half, z, own] = self.kept[j, half, z, own] + self.recv1[j, half, z, own].astype(F32)

            self.give(q, 1 + half)
            self.send(q, 3 + half)

    def summed(self, j, half, z):
        return self.kept[j, half, z, self.own[half]] + self.recv2[j, half, z].astype(F32)

    def third(self, q):
        j = lax.rem(q, self.slots)
        self.wait(q, 3, 4)

        @loop(len(OTHERS))
        def _(d):
            z = lax.rem(self.at.z + d + 1, LINE)
            for half in PAIR:
                self.snd3[j, d, :, self.cols(half)] = self.summed(j, half, z).astype(BF16)

        self.send(q, 5, 6, 7)

    def last(self, q):
        j = lax.rem(q, self.slots)
        totals = [self.summed(j, half, self.at.z) for half in PAIR]
        self.wait(q, 5, 6, 7)
        for d in OTHERS:
            totals = [total + self.recv3[j, d, :, self.cols(half)].astype(F32) for half, total in enumerate(totals)]
        self.give(q, 3, 4, 5, 6, 7)
        return totals


def ring_scratch(slots, rows, width):
    half = width // 2
    return [
        pltpu.VMEM((2, 4, 2, 2, 2, rows, width), F32),
        pltpu.VMEM((2, 4, 2, 2, rows, width), F32),
        pltpu.VMEM((slots, 2, 4, 2, rows, half), F32),
    ] + [pltpu.VMEM((slots, 2, 4, 2, rows, half), BF16)] * 2 + [pltpu.VMEM((slots, 2, 4, rows, half), BF16)] * 2 + [
        pltpu.VMEM((slots, 3, rows, width), BF16)] * 2 + [DMA_SEM((slots, 16))] * 2 + [
        pltpu.SemaphoreType.REGULAR((slots, 8))]


CHUNKS = 8
RING = 12
SUMS = 5
QUICK = 4
SPREAD_LAGS = (1, 2, 3, 4, 6, 7, 8, 9)
RING_LAGS = (1, 3, 5, 8)


def step_kernel(
        total_rows, lam_ref, feat_a, feat_b, w_one, w_two, w_three, gain_one, shift_one, gain_two, shift_two,
        grad_w_three, grad_w_two, grad_w_one, loss_total, total_two, total_one, saved_act, saved_norm,
        grad, pre, wide, turned, weight, normed, act, sides, side_sums, local, embed_local, embed_total, loss_local, mean_col, turned_sums, by_row, scales,
        wide_sem, w_sem, load_sem, out_sem, *scratch):
    at = Place()
    place = (at.z, at.y, at.x, at.core)

    def spread(q, stage):
        cols = ring.cols((stage - 1) % 2)
        if stage < 11:
            here, peer = wide.at[(q, *place)], at.z_peers[stage - 8]
        elif stage == 11:
            here, peer = wide.at[q, :, at.y, at.x, at.core, :, cols], at.y_peer
        elif stage == 12:
            here, peer = wide.at[q, :, at.y, at.x, at.core, :, cols], at.x_peer
        elif stage == 13:
            here, peer = wide.at[q, :, :, at.x, at.core, :, cols], at.x_peer
        elif stage == 14:
            here, peer = wide.at[q, :, at.y, :, at.core, :, cols], at.y_peer
        else:
            here, peer = wide.at[q, :, :, :, at.core], at.partner
        return here, here, peer

    ring = Ring(at, 4 * CHUNKS, spread, *scratch[:RING])
    rows_dev, dim = grad.shape
    width = dim // CHUNKS
    view_rows = rows_dev // 2
    block_rows = min(64, view_rows)
    quarter = dim // 4
    count = 1.0 / total_rows
    weights = [w_one, w_two, w_three]
    gains, shifts = [gain_one, gain_two], [shift_one, shift_two]
    outs = [grad_w_three, grad_w_two, grad_w_one]
    totals = [embed_total, total_two, total_one]
    views = [pl.ds(v * view_rows, view_rows) for v in PAIR]
    rest = list(scratch[RING:])

    def take(number):
        taken, rest[:] = rest[:number], rest[number:]
        return taken

    top = pl.ds(0, 2)
    side = [[QuickSums(at, (sides, (layer, v, top)), (side_sums, (layer, v, top)), *take(QUICK)) for v in PAIR] for layer in OTHERS]
    pair_sums = QuickSums(at, (sides, (0, 0)), (side_sums, (0, 0)), *take(QUICK))
    loss_sums = QuickSums(at, (loss_local, ...), (loss_total, ...), *take(QUICK))
    sums = [[Sums(at, (embed_local, ()), (embed_total, ()), *take(SUMS))]]
    for layer in PAIR:
        sums.append([Sums(at, (local, (layer, h)), (totals[layer + 1], (h,)), *take(SUMS)) for h in PAIR])

    def act_copy(layer):
        return pltpu.make_async_copy(saved_act.at[1 - layer], act, load_sem.at[0])

    def norm_copy(layer):
        return pltpu.make_async_copy(saved_norm.at[1 - layer], normed.at[layer], load_sem.at[1])

    def feat_copy(v):
        return pltpu.make_async_copy((feat_a, feat_b)[v], normed.at[0, views[v]], load_sem.at[v])

    def wide_copy(layer, n):
        cols = pl.ds(pl.multiple_of(n * width, width), width)
        return pltpu.make_async_copy(weights[layer].at[:, :, :, :, :, cols], wide.at[n], wide_sem.at[n])

    feat_copy(0).start()
    lead = 4
    for n in range(lead):
        wide_copy(0, n).start()
    feat_copy(1).start()
    puts = {}

    def put(name, v, src, dst, k):
        copy = pltpu.make_async_copy(src, dst, out_sem.at[k, v])
        copy.start()
        puts[name, v] = copy

    def drain(*names):
        for name in names:
            for v in PAIR:
                puts.pop((name, v)).wait()

    def matmul(layer, v, hook, step):
        @loop(CHUNKS // 2)
        def _(m):
            if step:
                pl.when(m == hook)(step)
            chunks = [2 * m, 2 * m + 1]
            if v == 0:
                if layer == 0:
                    for n in chunks:
                        pl.when(n + lead < CHUNKS)(lambda n=n: wide_copy(0, n + lead).start())
                for n in chunks:
                    wide_copy(layer, n).wait()
            elif layer < 2:
                for n in chunks:
                    pl.when(m > 0)(lambda n=n: wide_copy(layer + 1, n - 2).start())
            for n in chunks:
                cols = pl.ds(pl.multiple_of(n * width, width), width)
                out = jnp.dot(normed[layer % 2, views[v]], wide[n].reshape(dim, width), preferred_element_type=F32)
                pre[views[v], cols] = out
                sides[layer, v, FIRST, cols] = col_sum(out)
                sides[layer, v, SECOND, cols] = col_sum(out * out)

        if v and layer < 2:
            for n in PAIR:
                wide_copy(layer + 1, CHUNKS - 2 + n).start()
        side[layer][v].begin()

    def normalise(layer, v):
        side[layer][v].arrive()
        mean = side_sums[layer, v, FIRST, :] / total_rows
        inv = lax.rsqrt(side_sums[layer, v, SECOND, :] / total_rows - mean * mean + NORM_EPS)
        scales[2 - layer, v:v + 1, :] = gains[layer][...] * inv if layer < 2 else inv
        sides[layer, v, FIRST, :] = mean
        sides[layer, v, SECOND, :] = inv

        @loop(CHUNKS)
        def _(n):
            cols = pl.ds(pl.multiple_of(n * width, width), width)
            mean, inv = sides[layer, v, FIRST, cols], sides[layer, v, SECOND, cols]
            if layer < 2:
                gain, shift = gains[layer][:, cols], shifts[layer][:, cols]

            @loop(view_rows // block_rows)
            def _(r):
                rows = pl.ds(pl.multiple_of(v * view_rows + r * block_rows, block_rows), block_rows)
                value = (pre[rows, cols] - mean) * inv
                if layer < 2:
                    grad[rows, cols] = value.astype(BF16)
                    value = jnp.maximum(gain * value + shift, 0.0)
                normed[(layer + 1) % 2, rows, cols] = value.astype(BF16)

        if layer < 2:
            put(("act", layer), v, normed.at[(layer + 1) % 2, views[v]], saved_act.at[layer, views[v]], layer)
            put(("norm", layer), v, grad.at[views[v]], saved_norm.at[layer, views[v]], 2)

    def turn(src, dst, first, v):
        part = view_rows // 2

        @loop(CHUNKS)
        def _(n):
            cols = pl.ds(pl.multiple_of(n * width, width), width)
            for k in PAIR:
                block = src[pl.ds(v * view_rows + k * part, part), cols].T
                dst[first + 2 * v + k, lax.div(n, 2), lax.rem(n, 2)] = block.reshape(dst.shape[3:])

    enter(at.z_peers + at.cube_peers)
    feat_copy(0).wait()
    matmul(0, 0, 0, None)
    feat_copy(1).wait()
    matmul(0, 1, 3, side[0][0].over_plane)
    for v in PAIR:
        turn(normed.at[0], turned, 0, v)
    normalise(0, 0)
    for layer in PAIR:
        matmul(layer + 1, 0, 0, side[layer][1].over_plane)
        normalise(layer, 1)
        matmul(layer + 1, 1, 3, side[layer + 1][0].over_plane)
        if layer == 0:
            drain(("norm", 0))
        else:
            drain(("act", 0))
        normalise(layer + 1, 0)
    side[2][1].over_plane()
    normalise(2, 1)

    drain(("act", 1), ("norm", 1))
    act_copy(0).start()
    slots = weight.shape[0]

    def weight_copy(layer, n):
        slot = lax.rem(n, slots)
        return pltpu.make_async_copy(weights[2 - layer].at[lax.div(n, 2), lax.rem(n, 2)], weight.at[slot], w_sem.at[slot])

    for n in range(slots):
        weight_copy(0, n).start()

    lam = lam_ref[0]
    lane = 128
    block_rows_dev = ring.snd1.shape[-2]
    first_row = (((at.z * 2 + at.y) * 2 + at.x) * 2 + at.core) * block_rows_dev

    def pair_rows():
        @loop(CHUNKS)
        def _(n):
            cols = pl.ds(pl.multiple_of(n * width, width), width)
            one, two = [normed[1, views[v], cols].astype(F32) for v in PAIR]
            sides[0, 0, FIRST, cols] = col_sum(one)
            sides[0, 0, SECOND, cols] = col_sum(two)
            sides[0, 0, THIRD, cols] = col_sum(one * two)
            sides[0, 0, FOURTH, cols] = jnp.zeros((1, width), F32)
            pre[views[0], cols] = jnp.zeros((view_rows, width), F32)

        by_row[...] = jnp.zeros_like(by_row)
        pair_sums.begin()

    block = pl.ds(pl.multiple_of(lax.div(first_row, lane) * lane, lane), lane)
    part = lax.rem(first_row, lane)

    def keep_means():
        pair_sums.arrive()
        turned_sums[...] = jnp.broadcast_to(side_sums[0, 0, FIRST, block], (lane, lane)).T
        mean_col[...] = turned_sums[pl.ds(pl.multiple_of(part, 8), block_rows_dev), :]

    def row_sums():
        for k, row in enumerate((FIRST, THIRD)):
            sums_here = col_sum(by_row[k].T)
            spread = jnp.concatenate([sums_here] * (lane // block_rows_dev), axis=1)
            position = lax.broadcasted_iota(jnp.int32, spread.shape, 1)
            mine = (position >= part) & (position < part + block_rows_dev)
            embed_local[row, :] = jnp.zeros((1, dim), F32)
            embed_local[row, block] = jnp.where(mine, spread, 0.0)


    def chunk_cols(q):
        return pl.ds(pl.multiple_of(q * width, width), width)

    def correlate(q):
        @loop(LINE)
        def _(z):
            rows = pl.ds(pl.multiple_of(z * quarter, quarter), quarter)
            out = lax.dot_general(normed[1, views[0], rows], normed[1, views[1], chunk_cols(q)], DEPTH_DIMS,
                                  preferred_element_type=F32)
            ring.part[lax.rem(q, 2), z] = out.reshape(ring.part.shape[2:])

        ring.pair(q)

    def spread_line(q):
        for half, total in enumerate(ring.last(q)):
            start = q * width + half * ring.half
            row = first_row + lax.broadcasted_iota(jnp.int32, total.shape, 0)
            col = start + lax.broadcasted_iota(jnp.int32, total.shape, 1)
            diag = row == col
            cols = pl.ds(pl.multiple_of(start, ring.half), ring.half)
            total = jnp.where(diag, side_sums[0, 0, THIRD, cols], total)
            corr = total * count
            gap = 1.0 - corr
            loss_local[:, cols] = col_sum(jnp.where(diag, gap * gap, lam * corr * corr))
            slope = (jnp.where(diag, -2.0 * gap, 2.0 * lam * corr) * count).astype(BF16)
            wide[(q, *place, ALL, ring.cols(half))] = slope
            slope = slope.astype(F32)
            embed_local[SECOND, cols] = col_sum(slope * mean_col[:, :ring.half])
            embed_local[FOURTH, cols] = col_sum(slope * total)
            terms = [slope * side_sums[0, 0, SECOND, cols], slope * total]
            for k, term in enumerate(terms):
                by_row[k] = by_row[k] + term
        ring.start(q, 8, 9, 10)

    def spread_one(q):
        ring.wait(q, 8, 9, 10)
        ring.start(q, 11, 12)

    def spread_two(q):
        ring.wait(q, 11, 12)
        ring.start(q, 13, 14)

    def spread_pair(q):
        ring.wait(q, 13, 14)
        ring.start(q, 15)

    def embed_grad(q):
        ring.wait(q, 15)
        cols = chunk_cols(q)
        pre[views[1], cols] = jnp.dot(normed[1, views[0]], wide[q].reshape(dim, width), preferred_element_type=F32)

        @loop(LINE)
        def _(z):
            into = pl.ds(pl.multiple_of(z * quarter, quarter), quarter)
            rows = lax.dot_general(normed[1, views[1], cols], wide[q, z].reshape(quarter, width), LANE_DIMS,
                                   preferred_element_type=F32)
            pre[views[0], into] = pre[views[0], into] + rows

    first_sums = sums[0][0]
    steps = (ring.first, ring.second, ring.third, spread_line, spread_one, spread_two, spread_pair, embed_grad)
    done = CHUNKS + SPREAD_LAGS[3]

    def start_sums():
        row_sums()
        first_sums.begin()

    def turn_two():
        for v in PAIR:
            turn(normed.at[0], wide, 0, v)
        norm_copy(0).start()

    moves = ((0, pair_rows), (1, pair_sums.over_plane), (3, keep_means), (done, start_sums), (done + 1, first_sums.over_plane),
             (done + 2, first_sums.over_line), (done + 3, first_sums.over_pair))

    @loop(CHUNKS + SPREAD_LAGS[-1])
    def _(t):
        pl.when(t < CHUNKS)(lambda: correlate(t))
        for when, move in moves:
            pl.when(t == when)(move)
        for step, lag in zip(steps, SPREAD_LAGS):
            pl.when((t >= lag) & (t < lag + CHUNKS))(lambda step=step, lag=lag: step(t - lag))
        pl.when(t == SPREAD_LAGS[-1] + LINE)(turn_two)

    loss_sums.begin()

    def finish_grad(layer, j):
        cols = chunk_cols(j)
        per = CHUNKS // 2
        total, sel = (embed_total, cols) if layer == 0 else (totals[layer].at[lax.div(j, per)], chunk_cols(lax.rem(j, per)))
        for v in PAIR:
            mean0 = total[v:v + 1, sel] * count
            mean1 = total[2 + v:3 + v, sel] * count
            scale = scales[layer, v:v + 1, cols]

            @loop(view_rows // block_rows)
            def _(r):
                rows = pl.ds(pl.multiple_of(v * view_rows + r * block_rows, block_rows), block_rows)
                xhat = normed[(layer + 1) % 2, rows, cols].astype(F32)
                grad[rows, cols] = (scale * (pre[rows, cols] - (mean0 + xhat * mean1))).astype(BF16)

    def weight_grad(layer, j):
        q = (layer + 1) * CHUNKS + j
        source, first = (turned, 0) if layer == 2 else (wide, LINE * layer)

        @loop(2)
        def _(p):
            span = pl.ds(2 * p, 2)
            feed = jnp.concatenate([source[first + k, span].reshape(2 * quarter, -1) for k in range(LINE)], axis=1)
            out = jnp.dot(feed, grad[:, chunk_cols(j)], preferred_element_type=F32)
            ring.part[lax.rem(q, 2), span] = out.reshape(2, *ring.part.shape[2:])

        ring.pair(q)

    def input_grad(layer, n):
        cols = chunk_cols(n)
        weight_copy(layer, n).wait()
        half = local.at[layer, lax.div(n, CHUNKS // 2)]
        sel = chunk_cols(lax.rem(n, CHUNKS // 2))

        @loop(2)
        def _(v):
            rows = pl.ds(pl.multiple_of(v * view_rows, view_rows), view_rows)
            out = lax.dot_general(grad[rows, :], weight[lax.rem(n, slots)].reshape(width, dim), LANE_DIMS,
                                  preferred_element_type=F32)
            out = jnp.where(act[rows, cols] > 0, out, 0.0)
            pre[rows, cols] = out
            half[pl.ds(v, 1), sel] = col_sum(out)
            half[pl.ds(2 + v, 1), sel] = col_sum(out * normed[layer % 2, rows, cols].astype(F32))

        pl.when(n + slots < CHUNKS)(lambda: weight_copy(layer, n + slots).start())

    def serve(layer, j):
        t = layer * CHUNKS + j
        for step, lag in zip((ring.first, ring.second, ring.third), RING_LAGS):
            pl.when((t >= lag) & (t < lag + 3 * CHUNKS))(lambda step=step, lag=lag: step(CHUNKS + t - lag))
        if layer:
            for half, block in enumerate(ring.last(t)):
                outs[layer - 1][:, pl.ds(pl.multiple_of(j * width + half * ring.half, ring.half), ring.half)] = block

    for layer in OTHERS:
        old, new = sums[layer], sums[layer + 1] if layer < 2 else None
        old[0].arrive()

        def settle():
            if layer:
                old[1].arrive()

            @pl.loop(3, CHUNKS)
            def _(k):
                finish_grad(layer, k)

            if layer == 0:
                norm_copy(1).start()

        def late_loads():
            new[1].begin()
            if layer == 0:
                act_copy(1).start()
                for n in range(slots):
                    weight_copy(1, n).start()

        def relay_pair():
            new[0].over_pair()
            new[1].over_plane()

        before, middle, after = [], [(2, settle)], []
        if layer:
            middle.append((0, old[1].over_pair))
        if layer == 0:
            before.append((3, lambda: act_copy(0).wait()))
        if new:
            before += [(2, lambda: norm_copy(layer).wait()), (5, new[0].over_plane), (6, new[0].over_line), (7, relay_pair)]
            after += [(4, new[0].begin), (6, late_loads), (7, new[1].over_line)]

        @loop(CHUNKS)
        def _(j):
            for when, move in before:
                pl.when(j == when)(move)
            pl.when(j < 3)(lambda: finish_grad(layer, j))
            weight_grad(layer, j)
            for when, move in middle:
                pl.when(j == when)(move)
            if new:
                @pl.when((j > 2) & (j < 7))
                def _():
                    @loop(2)
                    def _(k):
                        input_grad(layer, 2 * (j - 3) + k)
            for when, move in after:
                pl.when(j == when)(move)
            serve(layer, j)

        if layer == 0:
            act_copy(1).wait()
            for v in PAIR:
                turn(act, wide, LINE, v)
            loss_sums.over_plane()

    @loop(CHUNKS)
    def _(j):
        serve(len(OTHERS), j)

    loss_sums.arrive()


def step(total_rows, vmem, lam, feat_a, feat_b, weights, vectors):
    view_rows, dim = feat_a.shape
    rows, width, blocks = 2 * view_rows, dim // CHUNKS, dim // 32
    hbm = pl.BlockSpec(memory_space=pl.ANY)
    vm = pl.BlockSpec(memory_space=pltpu.VMEM)
    cube = (LINE, 2, 2, 2, blocks)
    scratch = [
        pltpu.VMEM((rows, dim), BF16),
        pltpu.VMEM((rows, dim), F32),
        pltpu.VMEM((CHUNKS, *cube, width), BF16),
        pltpu.VMEM((LINE, *cube, view_rows // 2), BF16),
        pltpu.VMEM((3, 2, 2, blocks, dim), BF16),
        pltpu.VMEM((2, rows, dim), BF16),
        pltpu.VMEM((rows, dim), BF16),
        pltpu.VMEM((3, 2, 4, dim), F32),
        pltpu.VMEM((3, 2, 4, dim), F32),
        pltpu.VMEM((2, 2, 4, dim // 2), F32),
        pltpu.VMEM((4, dim), F32),
        pltpu.VMEM((4, dim), F32),
        pltpu.VMEM((1, dim), F32),
        pltpu.VMEM((blocks, 128), F32),
        pltpu.VMEM((128, 128), F32),
        pltpu.VMEM((2, blocks, width // 2), F32),
        pltpu.VMEM((3, 2, dim), F32),
        DMA_SEM((CHUNKS,)),
        DMA_SEM((3,)),
        DMA_SEM((3,)),
        DMA_SEM((3, 2)),
    ] + ring_scratch(CHUNKS, blocks, width)
    for _ in range(6):
        scratch += quick_scratch(2, dim)
    scratch += quick_scratch(4, dim) + quick_scratch(1, dim) + sums_scratch(4, dim)
    for _ in range(4):
        scratch += sums_scratch(4, dim // 2)
    halves = jax.ShapeDtypeStruct((2, 4, dim // 2), F32)
    saved = jax.ShapeDtypeStruct((2, rows, dim), BF16)
    return pl.pallas_call(
        functools.partial(step_kernel, total_rows),
        out_shape=[jax.ShapeDtypeStruct((blocks, dim), F32)] * 3 + [
            jax.ShapeDtypeStruct((1, dim), F32), halves, halves, saved, saved],
        in_specs=[pl.BlockSpec(memory_space=pltpu.SMEM)] + [hbm] * 5 + [vm] * 4,
        out_specs=[vm] * 6 + [hbm] * 2,
        scratch_shapes=scratch,
        compiler_params=pltpu.CompilerParams(collective_id=0, has_side_effects=True, vmem_limit_bytes=vmem),
    )(lam.reshape(1), feat_a, feat_b, *[weight.reshape(*cube, dim) for weight in weights],
      *[value.reshape(1, dim) for value in vectors])


def finish_kernel(total_two, total_one, loss_cols, *refs):
    gain_one, shift_one, gain_two, shift_two, loss = refs[6:]
    for grad, out in zip(refs[:3], refs[3:6]):
        out[...] = grad[...]
    half = total_two.shape[-1]
    for total, gain, shift in ((total_two, gain_two, shift_two), (total_one, gain_one, shift_one)):
        for h in PAIR:
            cols = pl.ds(h * half, half)
            shift[:, cols] = total[h, FIRST] + total[h, SECOND]
            gain[:, cols] = total[h, THIRD] + total[h, FOURTH]
    loss[...] = jnp.sum(loss_cols[...], axis=1, keepdims=True)


def finish(total_two, total_one, loss_cols, grads):
    vm = pl.BlockSpec(memory_space=pltpu.VMEM)
    row = jax.ShapeDtypeStruct((1, loss_cols.shape[1]), F32)
    outs = pl.pallas_call(
        finish_kernel,
        out_shape=[jax.ShapeDtypeStruct(grad.shape, F32) for grad in grads] + [row] * 4 + [jax.ShapeDtypeStruct((1, 1), F32)],
        in_specs=[vm] * 6,
        out_specs=[vm] * 8,
    )(total_two, total_one, loss_cols, *grads)
    return outs[:3], [row.reshape(-1) for row in outs[3:7]], outs[7].reshape(())


def solution(mesh):
    shards = mesh.shape["data"]

    def local_step(h_a, h_b, w_one, w_two, w_three, gain_one, shift_one, gain_two, shift_two, lam_off):
        rows_dev = h_a.shape[0]
        total_rows = rows_dev * shards
        grad_w_three, grad_w_two, grad_w_one, loss_cols, total_two, total_one = step(
            total_rows, 67000000, lam_off, h_a, h_b, (w_one, w_two, w_three),
            (gain_one, shift_one, gain_two, shift_two))[:6]
        grads, vectors, loss_total = finish(total_two, total_one, loss_cols, [grad_w_one, grad_w_two, grad_w_three])
        return (loss_total, *grads, *vectors)

    row_spec = P("data", None)
    whole_mat = P(None, None)
    whole_vec = P(None)
    return jax.shard_map(
        local_step, mesh=mesh,
        in_specs=(row_spec, row_spec, whole_mat, whole_mat, whole_mat,
                  whole_vec, whole_vec, whole_vec, whole_vec, P()),
        out_specs=(P(), row_spec, row_spec, row_spec, whole_vec, whole_vec, whole_vec, whole_vec),
        check_vma=False)
```

profile of v0, /device:TPU:0, one launch (start us, length us, event | category | flops | bytes accessed | tf_op | source)
XLA Modules:
  0.0 288.4 jit_solution(15731840058149478285)
XLA Ops:
  1.3 284.5 %shard_map.161 = (f32[64,2048]{1,0:T(8,128)}, f32[64,2048]{1,0:T(8,128)}, f32[64,2048]{1,0:T(8,128)}, f32[1,2048]{1,0:T(1,128)}, f32[2,4,1024]{2,1,0:T(4,128)}, ...) custom-call(f32[1]{0:T(128)} %bitcast.13.lam_ref, bf16[512,2048]{1,0:T(8,128)(2,1)} %feat_a.1, ...), custom_call_target="tpu_custom_call" | custom-call | tf_op jit(solution)/shard_map/pallas_call | solution.py:762
  285.8 2.6 shard_map.162
where the time goes:
time: 289 us; the launch traced here: 288 us
  Pallas kernels  287 us (99%)
    pallas_call x1, Pallas kernels, step(): pl.pallas_call(functools.partial(step_kernel, total_rows), out_shape=[jax...  285 us

commit v1 on v0

--- a/solution.py
+++ b/solution.py
@@ -333,7 +333,7 @@
     rows_dev, dim = grad.shape
     width = dim // CHUNKS
     view_rows = rows_dev // 2
-    block_rows = min(64, view_rows)
+    block_rows = min(128, view_rows)
     quarter = dim // 4
     count = 1.0 / total_rows
     weights = [w_one, w_two, w_three]
@@ -386,11 +386,11 @@
                 puts.pop((name, v)).wait()
 
     def matmul(layer, v, hook, step):
-        @loop(CHUNKS // 2)
+        @loop(CHUNKS // LINE)
         def _(m):
             if step:
                 pl.when(m == hook)(step)
-            chunks = [2 * m, 2 * m + 1]
+            chunks = [LINE * m + k for k in range(LINE)]
             if v == 0:
                 if layer == 0:
                     for n in chunks:
@@ -399,7 +399,7 @@
                     wide_copy(layer, n).wait()
             elif layer < 2:
                 for n in chunks:
-                    pl.when(m > 0)(lambda n=n: wide_copy(layer + 1, n - 2).start())
+                    pl.when(m > 0)(lambda n=n: wide_copy(layer + 1, n - LINE).start())
             for n in chunks:
                 cols = pl.ds(pl.multiple_of(n * width, width), width)
                 out = jnp.dot(normed[layer % 2, views[v]], wide[n].reshape(dim, width), preferred_element_type=F32)
@@ -408,8 +408,8 @@
                 sides[layer, v, SECOND, cols] = col_sum(out * out)
 
         if v and layer < 2:
-            for n in PAIR:
-                wide_copy(layer + 1, CHUNKS - 2 + n).start()
+            for n in range(LINE):
+                wide_copy(layer + 1, LINE + n).start()
         side[layer][v].begin()
 
     def normalise(layer, v):
@@ -454,14 +454,14 @@
     feat_copy(0).wait()
     matmul(0, 0, 0, None)
     feat_copy(1).wait()
-    matmul(0, 1, 3, side[0][0].over_plane)
+    matmul(0, 1, 1, side[0][0].over_plane)
     for v in PAIR:
         turn(normed.at[0], turned, 0, v)
     normalise(0, 0)
     for layer in PAIR:
         matmul(layer + 1, 0, 0, side[layer][1].over_plane)
         normalise(layer, 1)
-        matmul(layer + 1, 1, 3, side[layer + 1][0].over_plane)
+        matmul(layer + 1, 1, 1, side[layer + 1][0].over_plane)
         if layer == 0:
             drain(("norm", 0))
         else:
@@ -569,10 +569,10 @@
         cols = chunk_cols(q)
         pre[views[1], cols] = jnp.dot(normed[1, views[0]], wide[q].reshape(dim, width), preferred_element_type=F32)
 
-        @loop(LINE)
-        def _(z):
-            into = pl.ds(pl.multiple_of(z * quarter, quarter), quarter)
-            rows = lax.dot_general(normed[1, views[1], cols], wide[q, z].reshape(quarter, width), LANE_DIMS,
+        @loop(2)
+        def _(p):
+            into = pl.ds(pl.multiple_of(p * 2 * quarter, quarter), 2 * quarter)
+            rows = lax.dot_general(normed[1, views[1], cols], wide[q, pl.ds(2 * p, 2)].reshape(2 * quarter, width), LANE_DIMS,
                                    preferred_element_type=F32)
             pre[views[0], into] = pre[views[0], into] + rows
 

time: 289 us -> 285 us (0.986)
  Pallas kernels: 287 us -> 284 us
    pallas_call x1, Pallas kernels: 285 us -> 281 us  [step(): pl.pallas_call(functools.partial(step_kernel, total_rows), out_shape=[jax...]
where the time goes in v1:
time: 285 us
  Pallas kernels  284 us (100%)
    pallas_call x1, Pallas kernels, step(): pl.pallas_call(functools.partial(step_kernel, total_rows), out_shape=[jax...  281 us

profile of v1, /device:TPU:0, one launch (start us, length us, event | category | flops | bytes accessed | tf_op | source)
XLA Modules:
  0.0 285.1 jit_solution(16504223125852366015)
XLA Ops:
  1.3 281.2 %shard_map.161 = (f32[64,2048]{1,0:T(8,128)}, f32[64,2048]{1,0:T(8,128)}, f32[64,2048]{1,0:T(8,128)}, f32[1,2048]{1,0:T(1,128)}, f32[2,4,1024]{2,1,0:T(4,128)}, ...) custom-call(f32[1]{0:T(128)} %bitcast.13.lam_ref, bf16[512,2048]{1,0:T(8,128)(2,1)} %feat_a.1, ...), custom_call_target="tpu_custom_call" | custom-call | tf_op jit(solution)/shard_map/pallas_call | solution.py:762
  282.5 2.6 shard_map.162

commit v2 on v1

--- a/solution.py
+++ b/solution.py
@@ -301,7 +301,7 @@
 RING = 12
 SUMS = 5
 QUICK = 4
-SPREAD_LAGS = (1, 2, 3, 4, 6, 7, 8, 9)
+SPREAD_LAGS = (1, 2, 3, 4, 6, 7, 9, 10)
 RING_LAGS = (1, 3, 5, 8)
 
 
@@ -467,6 +467,15 @@
         else:
             drain(("act", 0))
         normalise(layer + 1, 0)
+    by_row[...] = jnp.zeros_like(by_row)
+    sides[0, 0, FOURTH, :] = jnp.zeros((1, dim), F32)
+
+    @loop(CHUNKS)
+    def _(n):
+        cols = pl.ds(pl.multiple_of(n * width, width), width)
+        sides[0, 0, FIRST, cols] = col_sum(normed[1, views[0], cols].astype(F32))
+        pre[views[0], cols] = jnp.zeros((view_rows, width), F32)
+
     side[2][1].over_plane()
     normalise(2, 1)
 
@@ -491,13 +500,9 @@
         def _(n):
             cols = pl.ds(pl.multiple_of(n * width, width), width)
             one, two = [normed[1, views[v], cols].astype(F32) for v in PAIR]
-            sides[0, 0, FIRST, cols] = col_sum(one)
             sides[0, 0, SECOND, cols] = col_sum(two)
             sides[0, 0, THIRD, cols] = col_sum(one * two)
-            sides[0, 0, FOURTH, cols] = jnp.zeros((1, width), F32)
-            pre[views[0], cols] = jnp.zeros((view_rows, width), F32)
-
-        by_row[...] = jnp.zeros_like(by_row)
+
         pair_sums.begin()
 
     block = pl.ds(pl.multiple_of(lax.div(first_row, lane) * lane, lane), lane)
@@ -589,7 +594,7 @@
             turn(normed.at[0], wide, 0, v)
         norm_copy(0).start()
 
-    moves = ((0, pair_rows), (1, pair_sums.over_plane), (3, keep_means), (done, start_sums), (done + 1, first_sums.over_plane),
+    moves = ((0, pair_rows), (2, pair_sums.over_plane), (4, keep_means), (done, start_sums), (done + 1, first_sums.over_plane),
              (done + 2, first_sums.over_line), (done + 3, first_sums.over_pair))
 
     @loop(CHUNKS + SPREAD_LAGS[-1])

time: 285 us -> 280 us (0.982)
  Pallas kernels: 284 us -> 278 us
    pallas_call x1, Pallas kernels: 281 us -> 276 us  [step(): pl.pallas_call(functools.partial(step_kernel, total_rows), out_shape=[jax...]
where the time goes in v2:
time: 280 us
  Pallas kernels  278 us (99%)
    pallas_call x1, Pallas kernels, step(): pl.pallas_call(functools.partial(step_kernel, total_rows), out_shape=[jax...  276 us

profile of v2, /device:TPU:0, one launch (start us, length us, event | category | flops | bytes accessed | tf_op | source)
XLA Modules:
  0.0 279.5 jit_solution(8836230951165756666)
XLA Ops:
  1.3 275.6 %shard_map.161 = (f32[64,2048]{1,0:T(8,128)}, f32[64,2048]{1,0:T(8,128)}, f32[64,2048]{1,0:T(8,128)}, f32[1,2048]{1,0:T(1,128)}, f32[2,4,1024]{2,1,0:T(4,128)}, ...) custom-call(f32[1]{0:T(128)} %bitcast.13.lam_ref, bf16[512,2048]{1,0:T(8,128)(2,1)} %feat_a.1, ...), custom_call_target="tpu_custom_call" | custom-call | tf_op jit(solution)/shard_map/pallas_call | solution.py:767
  276.9 2.6 shard_map.162

commit v3 on v2

--- a/solution.py
+++ b/solution.py
@@ -168,9 +168,7 @@
         pltpu.VMEM((rows, cols // 2), F32),
         pltpu.VMEM((4, rows, cols // 2), F32),
         pltpu.VMEM((4, rows, cols // 2), F32),
-        DMA_SEM((8,)),
-        DMA_SEM((8,)),
-    ]
+    ] + [DMA_SEM((CUBE,))] * 2
 
 
 class Ring:
@@ -459,7 +457,7 @@
         turn(normed.at[0], turned, 0, v)
     normalise(0, 0)
     for layer in PAIR:
-        matmul(layer + 1, 0, 0, side[layer][1].over_plane)
+        matmul(layer + 1, 0, 1, side[layer][1].over_plane)
         normalise(layer, 1)
         matmul(layer + 1, 1, 1, side[layer + 1][0].over_plane)
         if layer == 0:
@@ -574,7 +572,7 @@
         cols = chunk_cols(q)
         pre[views[1], cols] = jnp.dot(normed[1, views[0]], wide[q].reshape(dim, width), preferred_element_type=F32)
 
-        @loop(2)
+        @loop(len(PAIR))
         def _(p):
             into = pl.ds(pl.multiple_of(p * 2 * quarter, quarter), 2 * quarter)
             rows = lax.dot_general(normed[1, views[1], cols], wide[q, pl.ds(2 * p, 2)].reshape(2 * quarter, width), LANE_DIMS,
@@ -627,7 +625,7 @@
         q = (layer + 1) * CHUNKS + j
         source, first = (turned, 0) if layer == 2 else (wide, LINE * layer)
 
-        @loop(2)
+        @loop(len(PAIR))
         def _(p):
             span = pl.ds(2 * p, 2)
             feed = jnp.concatenate([source[first + k, span].reshape(2 * quarter, -1) for k in range(LINE)], axis=1)
@@ -636,23 +634,28 @@
 
         ring.pair(q)
 
-    def input_grad(layer, n):
-        cols = chunk_cols(n)
-        weight_copy(layer, n).wait()
-        half = local.at[layer, lax.div(n, CHUNKS // 2)]
-        sel = chunk_cols(lax.rem(n, CHUNKS // 2))
-
-        @loop(2)
+    def input_grad(layer, p):
+        two = 2 * width
+        cols = pl.ds(pl.multiple_of(p * two, two), two)
+        for n in PAIR:
+            weight_copy(layer, 2 * p + n).wait()
+        half = local.at[layer, lax.div(p, 2)]
+        sel = pl.ds(pl.multiple_of(lax.rem(p, 2) * two, two), two)
+
+        @loop(len(PAIR))
         def _(v):
             rows = pl.ds(pl.multiple_of(v * view_rows, view_rows), view_rows)
-            out = lax.dot_general(grad[rows, :], weight[lax.rem(n, slots)].reshape(width, dim), LANE_DIMS,
-                                  preferred_element_type=F32)
+            block = weight[pl.ds(2 * lax.rem(p, 2), 2)].reshape(two, dim)
+            out = lax.dot_general(grad[rows, :], block, LANE_DIMS, preferred_element_type=F32)
             out = jnp.where(act[rows, cols] > 0, out, 0.0)
             pre[rows, cols] = out
             half[pl.ds(v, 1), sel] = col_sum(out)
             half[pl.ds(2 + v, 1), sel] = col_sum(out * normed[layer % 2, rows, cols].astype(F32))
 
-        pl.when(n + slots < CHUNKS)(lambda: weight_copy(layer, n + slots).start())
+        @pl.when(p < 2)
+        def _():
+            for n in PAIR:
+                weight_copy(layer, 2 * p + n + slots).start()
 
     def serve(layer, j):
         t = layer * CHUNKS + j
@@ -706,11 +709,7 @@
             for when, move in middle:
                 pl.when(j == when)(move)
             if new:
-                @pl.when((j > 2) & (j < 7))
-                def _():
-                    @loop(2)
-                    def _(k):
-                        input_grad(layer, 2 * (j - 3) + k)
+                pl.when((j > 2) & (j < 7))(lambda: input_grad(layer, j - 3))
             for when, move in after:
                 pl.when(j == when)(move)
             serve(layer, j)
@@ -739,7 +738,7 @@
         pltpu.VMEM((rows, dim), F32),
         pltpu.VMEM((CHUNKS, *cube, width), BF16),
         pltpu.VMEM((LINE, *cube, view_rows // 2), BF16),
-        pltpu.VMEM((3, 2, 2, blocks, dim), BF16),
+        pltpu.VMEM((LINE, 2, 2, blocks, dim), BF16),
         pltpu.VMEM((2, rows, dim), BF16),
         pltpu.VMEM((rows, dim), BF16),
         pltpu.VMEM((3, 2, 4, dim), F32),
@@ -753,7 +752,7 @@
         pltpu.VMEM((2, blocks, width // 2), F32),
         pltpu.VMEM((3, 2, dim), F32),
         DMA_SEM((CHUNKS,)),
-        DMA_SEM((3,)),
+        DMA_SEM((LINE,)),
         DMA_SEM((3,)),
         DMA_SEM((3, 2)),
     ] + ring_scratch(CHUNKS, blocks, width)

time: 280 us -> 278 us (level)
  no operation moved by 1% of the time
where the time goes in v3:
time: 278 us
  Pallas kernels  276 us (99%)
    pallas_call x1, Pallas kernels, step(): pl.pallas_call(functools.partial(step_kernel, total_rows), out_shape=[jax...  274 us

profile of v3, /device:TPU:0, one launch (start us, length us, event | category | flops | bytes accessed | tf_op | source)
XLA Modules:
  0.0 277.6 jit_solution(1322744400546750369)
XLA Ops:
  1.3 273.7 %shard_map.161 = (f32[64,2048]{1,0:T(8,128)}, f32[64,2048]{1,0:T(8,128)}, f32[64,2048]{1,0:T(8,128)}, f32[1,2048]{1,0:T(1,128)}, f32[2,4,1024]{2,1,0:T(4,128)}, ...) custom-call(f32[1]{0:T(128)} %bitcast.13.lam_ref, bf16[512,2048]{1,0:T(8,128)(2,1)} %feat_a.1, ...), custom_call_target="tpu_custom_call" | custom-call | tf_op jit(solution)/shard_map/pallas_call | solution.py:766
  274.9 2.6 shard_map.162

commit v4 on v3

--- a/solution.py
+++ b/solution.py
@@ -187,7 +187,10 @@
 
     def copy(self, q, stage):
         j, s = lax.rem(q, self.slots), lax.rem(q, 2)
-        if stage > 7:
+        if stage % REST == 0:
+            z, peer = pl.ds(2 * (stage // REST), 2), self.at.partner
+            src, dst = self.part.at[s, z, :, :, 1 - self.at.core], self.recv0.at[s, z]
+        elif stage > 7:
             src, dst, peer = self.spread(q, stage)
         else:
             peer = self.peers[stage]
@@ -195,10 +198,8 @@
                 src, dst = self.snd3.at[j, stage - 5], self.recv3.at[j, stage - 5]
             elif stage > 2:
                 src, dst = self.snd2.at[j, stage - 3], self.recv2.at[j, stage - 3]
-            elif stage:
+            else:
                 src, dst = self.snd1.at[j, stage - 1], self.recv1.at[j, stage - 1]
-            else:
-                src, dst = self.part.at[s, :, :, :, 1 - self.at.core], self.recv0.at[s]
         return remote(src, dst, self.send_sem.at[j, stage], self.recv_sem.at[j, stage], peer)
 
     def start(self, q, *stages):
@@ -224,12 +225,9 @@
             pl.when(q + depth < self.total)(lambda: pl.semaphore_signal(
                 self.credit.at[lax.rem(q, depth), stage], inc=1, device_id=(self.givers[stage],), device_id_type=MESH))
 
-    def pair(self, q):
-        self.send(q, 0)
-
     def first(self, q):
         at, s, j = self.at, lax.rem(q, 2), lax.rem(q, self.slots)
-        self.wait(q, 0)
+        self.wait(q, 0, REST)
 
         @loop(LINE)
         def _(z):
@@ -286,18 +284,20 @@
 
 def ring_scratch(slots, rows, width):
     half = width // 2
+    box, pairs = (LINE, 2, 2), (slots, 2, LINE)
     return [
-        pltpu.VMEM((2, 4, 2, 2, 2, rows, width), F32),
-        pltpu.VMEM((2, 4, 2, 2, rows, width), F32),
-        pltpu.VMEM((slots, 2, 4, 2, rows, half), F32),
-    ] + [pltpu.VMEM((slots, 2, 4, 2, rows, half), BF16)] * 2 + [pltpu.VMEM((slots, 2, 4, rows, half), BF16)] * 2 + [
-        pltpu.VMEM((slots, 3, rows, width), BF16)] * 2 + [DMA_SEM((slots, 16))] * 2 + [
+        pltpu.VMEM((2, *box, 2, rows, width), F32),
+        pltpu.VMEM((2, *box, rows, width), F32),
+        pltpu.VMEM((*pairs, 2, rows, half), F32),
+    ] + [pltpu.VMEM((*pairs, 2, rows, half), BF16)] * 2 + [pltpu.VMEM((*pairs, rows, half), BF16)] * 2 + [
+        pltpu.VMEM((slots, 3, rows, width), BF16)] * 2 + [DMA_SEM((slots, REST + 1))] * 2 + [
         pltpu.SemaphoreType.REGULAR((slots, 8))]
 
 
 CHUNKS = 8
 RING = 12
 SUMS = 5
+REST = 16
 QUICK = 4
 SPREAD_LAGS = (1, 2, 3, 4, 6, 7, 9, 10)
 RING_LAGS = (1, 3, 5, 8)
@@ -531,8 +531,9 @@
             out = lax.dot_general(normed[1, views[0], rows], normed[1, views[1], chunk_cols(q)], DEPTH_DIMS,
                                   preferred_element_type=F32)
             ring.part[lax.rem(q, 2), z] = out.reshape(ring.part.shape[2:])
-
-        ring.pair(q)
+            pl.when(z == 1)(lambda: ring.send(q, 0))
+
+        ring.start(q, REST)
 
     def spread_line(q):
         for half, total in enumerate(ring.last(q)):
@@ -602,7 +603,7 @@
             pl.when(t == when)(move)
         for step, lag in zip(steps, SPREAD_LAGS):
             pl.when((t >= lag) & (t < lag + CHUNKS))(lambda step=step, lag=lag: step(t - lag))
-        pl.when(t == SPREAD_LAGS[-1] + LINE)(turn_two)
+        pl.when(t == SPREAD_LAGS[-1] + LINE - 1)(turn_two)
 
     loss_sums.begin()
 
@@ -631,8 +632,9 @@
             feed = jnp.concatenate([source[first + k, span].reshape(2 * quarter, -1) for k in range(LINE)], axis=1)
             out = jnp.dot(feed, grad[:, chunk_cols(j)], preferred_element_type=F32)
             ring.part[lax.rem(q, 2), span] = out.reshape(2, *ring.part.shape[2:])
-
-        ring.pair(q)
+            pl.when(p == 0)(lambda: ring.send(q, 0))
+
+        ring.start(q, REST)
 
     def input_grad(layer, p):
         two = 2 * width

time: 278 us -> 277 us (level)
  no operation moved by 1% of the time
where the time goes in v4:
time: 277 us; the launch traced here: 276 us
  Pallas kernels  275 us (99%)
    pallas_call x1, Pallas kernels, step(): pl.pallas_call(functools.partial(step_kernel, total_rows), out_shape=[jax...  272 us

profile of v4, /device:TPU:0, one launch (start us, length us, event | category | flops | bytes accessed | tf_op | source)
XLA Modules:
  0.0 276.3 jit_solution(7721452484134175689)
XLA Ops:
  1.3 272.4 %shard_map.161 = (f32[64,2048]{1,0:T(8,128)}, f32[64,2048]{1,0:T(8,128)}, f32[64,2048]{1,0:T(8,128)}, f32[1,2048]{1,0:T(1,128)}, f32[2,4,1024]{2,1,0:T(4,128)}, ...) custom-call(f32[1]{0:T(128)} %bitcast.13.lam_ref, bf16[512,2048]{1,0:T(8,128)(2,1)} %feat_a.1, ...), custom_call_target="tpu_custom_call" | custom-call | tf_op jit(solution)/shard_map/pallas_call | solution.py:768
  273.7 2.6 shard_map.162

commit v5 on v4

--- a/solution.py
+++ b/solution.py
@@ -593,7 +593,7 @@
             turn(normed.at[0], wide, 0, v)
         norm_copy(0).start()
 
-    moves = ((0, pair_rows), (2, pair_sums.over_plane), (4, keep_means), (done, start_sums), (done + 1, first_sums.over_plane),
+    moves = ((3, pair_sums.over_plane), (4, keep_means), (done, start_sums), (done + 1, first_sums.over_plane),
              (done + 2, first_sums.over_line), (done + 3, first_sums.over_pair))
 
     @loop(CHUNKS + SPREAD_LAGS[-1])
@@ -603,6 +603,7 @@
             pl.when(t == when)(move)
         for step, lag in zip(steps, SPREAD_LAGS):
             pl.when((t >= lag) & (t < lag + CHUNKS))(lambda step=step, lag=lag: step(t - lag))
+        pl.when(t == 1)(pair_rows)
         pl.when(t == SPREAD_LAGS[-1] + LINE - 1)(turn_two)
 
     loss_sums.begin()

time: 277 us -> 275 us (level)
  no operation moved by 1% of the time
where the time goes in v5:
time: 275 us
  Pallas kernels  274 us (100%)
    pallas_call x1, Pallas kernels, step(): pl.pallas_call(functools.partial(step_kernel, total_rows), out_shape=[jax...  271 us

profile of v5, /device:TPU:0, one launch (start us, length us, event | category | flops | bytes accessed | tf_op | source)
XLA Modules:
  0.0 274.9 jit_solution(5841184435917208286)
XLA Ops:
  1.3 271.0 %shard_map.161 = (f32[64,2048]{1,0:T(8,128)}, f32[64,2048]{1,0:T(8,128)}, f32[64,2048]{1,0:T(8,128)}, f32[1,2048]{1,0:T(1,128)}, f32[2,4,1024]{2,1,0:T(4,128)}, ...) custom-call(f32[1]{0:T(128)} %bitcast.13.lam_ref, bf16[512,2048]{1,0:T(8,128)(2,1)} %feat_a.1, ...), custom_call_target="tpu_custom_call" | custom-call | tf_op jit(solution)/shard_map/pallas_call | solution.py:769
  272.3 2.6 shard_map.162
